TPU v7x, 32 devices: a whole 2x2x4 slice. The times are simulated.
32 devices in a mesh: row: 8 (over y, x, core), shift: 4 (over z).
Axes of the slice: x: 2, y: 2, z: 4, core: 2. Of those that a mesh axis runs over, the one named last changes fastest.
Arguments:
- snapshots: bfloat16 [4096, 2, 128], P('row'), may hold values from -6 to 6
- tail_sensors: bfloat16 [128, 2, 128], replicated, may hold values from -6 to 6
- shift_offsets: int32 [12], P('shift'), may hold values from 0 to 128
- start_basis: float32 [64, 4096], P(None, 'row'), may hold values from -0.09375 to 0.09375
Outputs:
- covariance: float32 [4096, 4096], P('row', 'shift')
- signal_basis: float32 [64, 4096], P(None, 'row')
Inputs may be any that keep to these rules, and one draw needn't show every extreme that they name: `shift_offsets`: each shift's first sensor.
All inputs are finite; a program needn't handle non-finite values.
Results may differ from a plain program's by a relative error of at most 0.0031.
Values may be sent and summed in bfloat16 or wider, within the bound.
A program may use at most 64 MiB of HBM per device.

v0:
```python
import jax
import jax.numpy as jnp
from jax import lax
from jax.sharding import PartitionSpec as P

M = 4096
SNAPS = 128
ITERS = 2
half_root = 0.7071067811865476


def make_some(extended, offset, start, count):
    window = lax.dynamic_slice_in_dim(extended, offset + start, count, 0).astype(jnp.float32)
    mirror = lax.dynamic_slice_in_dim(extended, offset + M - start - count, count, 0).astype(
        jnp.float32
    )[::-1]
    summed_pair = window + mirror
    difference = window - mirror
    upper_rows = jnp.concatenate([summed_pair[:, 0], summed_pair[:, 1]], axis=1)
    bottom = jnp.concatenate([difference[:, 1], -difference[:, 0]], axis=1)
    positions = start + jnp.arange(count, dtype=jnp.int32)
    chosen = jnp.where((positions < M // 2)[:, None], upper_rows, bottom)
    return (chosen * half_root).astype(jnp.bfloat16)


def factor(gram_matrix):
    lower_factor = jnp.linalg.cholesky(gram_matrix)
    identity = jnp.eye(gram_matrix.shape[0], dtype=jnp.float32)
    return jax.scipy.linalg.solve_triangular(lower_factor, identity, lower=True)


def per_device(snapshots, tail_sensors, shift_offsets, start_basis):
    block_rows = snapshots.shape[0]
    row_index = lax.axis_index("row")
    shift_index = lax.axis_index("shift")
    col_count = M // lax.axis_size("shift")
    normalizer = 1.0 / (SNAPS * shift_offsets.shape[0] * lax.axis_size("shift"))
    gathered = lax.all_gather(snapshots, "row", axis=0, tiled=True)
    extended = jnp.concatenate([gathered, tail_sensors], 0)
    every_offset = lax.all_gather(shift_offsets, "shift", axis=0, tiled=True)
    row_start = row_index * block_rows
    col_start = shift_index * col_count

    def add_block(which, running):
        offset = every_offset[which]
        own_rows = make_some(extended, offset, row_start, block_rows)
        col_rows = make_some(extended, offset, col_start, col_count)
        return running + lax.dot_general(
            own_rows, col_rows, (((1,), (1,)), ((), ())), preferred_element_type=jnp.float32
        )

    summed_block = lax.fori_loop(
        0, every_offset.shape[0], add_block, jnp.zeros((block_rows, col_count), jnp.float32)
    )
    cov_out = summed_block * normalizer
    basis_rows = lax.all_gather(start_basis, "row", axis=1, tiled=True)
    own_basis = start_basis
    for sweep in range(ITERS):
        basis_cols = lax.dynamic_slice_in_dim(basis_rows, shift_index * col_count, col_count, 1)
        column_terms = lax.dot_general(
            basis_cols, cov_out, (((1,), (1,)), ((), ())), precision=lax.Precision.HIGHEST
        )
        mapped = lax.psum(column_terms, "shift")
        local_gram = jnp.dot(mapped, mapped.T, precision=lax.Precision.HIGHEST)
        gram_matrix = lax.psum(local_gram, "row")
        own_basis = jnp.dot(factor(gram_matrix), mapped, precision=lax.Precision.HIGHEST)
        if sweep + 1 < ITERS:
            basis_rows = lax.all_gather(own_basis, "row", axis=1, tiled=True)
    return (cov_out, own_basis)


def solution(mesh):
    in_specs = (P("row", None, None), P(), P("shift"), P(None, "row"))
    out_specs = (P("row", "shift"), P(None, "row"))
    return jax.shard_map(
        per_device, mesh=mesh, in_specs=in_specs, out_specs=out_specs, check_vma=False
    )
```

profile of v0, /device:TPU:0, one launch (start us, length us, event | category | flops | bytes accessed | tf_op | source)
XLA Modules:
  0.0 375.3 jit_solution(9196168970584460465)
XLA Ops:
  8.7 1.3 dynamic-slice
  11.5 9.9 %all-reduce = s32[12]{0:T(128)S(1)} all-reduce(s32[12]{0:T(128)S(1)} %dynamic-update-slice.2), channel_id=1, replica_groups=mesh['row'=8,'shift'=4] {'shift'}, use_global_device_ids=true, to_apply=%add | all-reduce | flops 12 | bytes 96
  21.4 19.0 %all-gather.4.cloned.1.call-done = bf16[4096,2,128]{2,1,0:T(2,128)(2,1)} async-done(((bf16[512,2,128]{2,1,0:T(2,128)(2,1)}), bf16[4096,2,128]{2,1,0:T(2,128)(2,1)}) %all-gather.4.cloned.1.call-update) | async-done | bytes 2097168 | tf_op jit(solution)/shard_map/all_gather | solution.py:38
  40.4 6.4 %pad_maximum_fusion = bf16[4224,2,128]{2,1,0:T(2,128)(2,1)S(1)} fusion(bf16[128,2,128]{2,1,0:T(2,128)(2,1)} %param.10, bf16[4096,2,128]{2,1,0:T(2,128)(2,1)} %all-gather.4.cloned.1.call-done), kind=kLoop, calls=%fused_computation.31 | loop fusion | flops 1081344 | bytes 4325376 | tf_op jit(solution)/shard_map/concatenate | solution.py:39
  46.8 1.6 copy.30
  48.4 143.1 %while.18 = (s32[]{:T(128)}, f32[512,1024]{1,0:T(8,128)}, s32[]{:T(128)}, s32[12]{0:T(128)S(1)}, bf16[4224,2,128]{2,0,1:T(8,128)(2,1)}, /*index=5*/s32[]{:T(128)...) while((s32[]{:T(128)}, f32[512,1024]{1,0:T(8,128)}, ...), condition=%wide.region_1.2_spmd.clone, body=%wide.region_0.1_spmd.clone.sunk | while | flops 273222688 | bytes 47713820 | solution.py:52
  59.1 1.3 copy-done.1
  71.0 1.3 copy-done.1
  82.9 1.3 copy-done.1
  94.9 1.3 copy-done.1
  106.8 1.3 copy-done.1
  118.7 1.3 copy-done.1
  130.6 1.3 copy-done.1
  142.6 1.3 copy-done.1
  154.5 1.3 copy-done.1
  166.4 1.3 copy-done.1
  178.3 1.3 copy-done.1
  190.3 1.3 copy-done.1
  191.6 1.8 broadcast_multiply_fusion
  193.4 4.0 %fusion.16 = f32[64,512]{1,0:T(8,128)} fusion(f32[512,1024]{1,0:T(8,128)S(1)} %broadcast_multiply_fusion, f32[64,4096]{1,0:T(8,128)} %all-gather.6.cloned.1.call-done, s32[]{:T(128)S(6)} %select_n.96), kind=kOutput, calls=%fused_computation.35 | convolution fusion | flops 402653184 | bytes 2490372 | tf_op jit(solution)/shard_map/dot_general | solution.py:60
  197.5 34.7 %all-reduce.4.cloned.1.call-done = f32[64,512]{1,0:T(8,128)} async-done(((f32[64,512]{1,0:T(8,128)}), f32[64,512]{1,0:T(8,128)}) %all-reduce.4.cloned.1.call-update) | async-done | bytes 131088 | tf_op jit(solution)/shard_map/psum | solution.py:63
  233.4 22.4 %psum.29 = f32[64,64]{0,1:T(8,128)S(1)} all-reduce(f32[64,64]{0,1:T(8,128)S(1)} %fusion.32), channel_id=1, replica_groups=mesh['row'=8,'shift'=4] {'row'}, use_global_device_ids=true, to_apply=%region_3.4 | all-reduce | flops 4096 | bytes 32768 | tf_op jit(solution)/shard_map/psum | solution.py:65
  255.9 5.8 %cholesky.44 = f32[64,64]{1,0:T(8,128)S(1)} custom-call(f32[64,64]{1,0:T(8,128)S(1)} %fusion.27), custom_call_target="Cholesky" | custom-call | tf_op jit(solution)/shard_map/jit(cholesky)/cholesky | solution.py:27
  263.1 4.9 %custom-call.7 = f32[1,64,64]{1,2,0:T(8,128)S(1)} custom-call(f32[1,64,64]{2,1,0:T(8,128)S(1)} %fusion.22), custom_call_target="InvertDiagBlocksLowerTriangular" | custom-call | tf_op jit(solution)/shard_map/jit(_solve_triangular)/triangular_solve | solution.py:29
  268.2 1.8 fusion.33
  270.1 22.3 %all-gather.8.cloned.1.call-done = f32[64,4096]{1,0:T(8,128)} async-done(((f32[64,512]{1,0:T(8,128)}), f32[64,4096]{1,0:T(8,128)}) %all-gather.8.cloned.1.call-update) | async-done | bytes 1048592 | tf_op jit(solution)/shard_map/all_gather | solution.py:68
  292.4 3.7 fusion.14
  296.2 34.8 %all-reduce.6.cloned.1.call-done = f32[64,512]{1,0:T(8,128)} async-done(((f32[64,512]{1,0:T(8,128)}), f32[64,512]{1,0:T(8,128)}) %all-reduce.6.cloned.1.call-update) | async-done | bytes 131088 | tf_op jit(solution)/shard_map/psum | solution.py:63
  332.2 22.4 %psum.31 = f32[64,64]{0,1:T(8,128)S(1)} all-reduce(f32[64,64]{0,1:T(8,128)S(1)} %fusion.34), channel_id=1, replica_groups=mesh['row'=8,'shift'=4] {'row'}, use_global_device_ids=true, to_apply=%region_7.10 | all-reduce | flops 4096 | bytes 32768 | tf_op jit(solution)/shard_map/psum | solution.py:65
  354.6 5.8 %cholesky.55 = f32[64,64]{1,0:T(8,128)S(1)} custom-call(f32[64,64]{1,0:T(8,128)S(1)} %fusion.25), custom_call_target="Cholesky" | custom-call | tf_op jit(solution)/shard_map/jit(cholesky)/cholesky | solution.py:27
  361.8 4.9 %custom-call.8 = f32[1,64,64]{1,2,0:T(8,128)S(1)} custom-call(f32[1,64,64]{2,1,0:T(8,128)S(1)} %fusion.23), custom_call_target="InvertDiagBlocksLowerTriangular" | custom-call | tf_op jit(solution)/shard_map/jit(_solve_triangular)/triangular_solve | solution.py:29
  367.0 1.8 fusion.35
  (282 shorter events, 109.5 us)
Async XLA Ops:
  7.2 33.2 %all-gather.4.cloned.1.call-start = ((), (), s32[]{:S(2)}) async-start(), calls=%async_computation | async-start | bytes 2359296 | tf_op jit(solution)/shard_map/all_gather | solution.py:38
  7.9 185.5 %all-gather.6.cloned.1.call-start = ((), (), s32[]{:S(2)}) async-start(), calls=%async_computation.1 | async-start | bytes 1179648 | tf_op jit(solution)/shard_map/all_gather | solution.py:56
  8.6 223.5 %all-reduce.4.cloned.1.call-start = ((), (), s32[]{:S(2)}) async-start(), calls=%async_computation.2 | async-start | bytes 262144 | tf_op jit(solution)/shard_map/psum | solution.py:63
  55.7 2.1 copy-start
  56.5 1.4 copy-start.3
  56.5 1.6 copy-start.4
  67.6 2.1 copy-start
  68.4 1.4 copy-start.3
  68.4 1.6 copy-start.4
  79.5 2.1 copy-start
  80.4 1.6 copy-start.4
  91.5 2.1 copy-start
  92.3 1.6 copy-start.4
  103.4 2.1 copy-start
  104.2 1.6 copy-start.4
  115.3 2.1 copy-start
  116.1 1.6 copy-start.4
  127.2 2.1 copy-start
  128.1 1.6 copy-start.4
  139.2 2.1 copy-start
  140.0 1.6 copy-start.4
  151.1 2.1 copy-start
  151.9 1.6 copy-start.4
  163.0 2.1 copy-start
  163.8 1.6 copy-start.4
  174.9 2.1 copy-start
  175.8 1.6 copy-start.4
  186.9 2.1 copy-start
  187.7 1.6 copy-start.4
  193.4 102.8 %copy-start.5 = (f32[512,1024]{1,0:T(8,128)}, f32[512,1024]{1,0:T(8,128)S(1)}, u32[]{:S(2)}) copy-start(f32[512,1024]{1,0:T(8,128)S(1)} %broadcast_multiply_fusion) | copy-start | bytes 6291460
  197.4 95.0 %all-gather.8.cloned.1.call-start = ((), (), s32[]{:S(2)}) async-start(), calls=%async_computation.3 | async-start | bytes 1179648 | tf_op jit(solution)/shard_map/all_gather | solution.py:68
  270.1 60.9 %all-reduce.6.cloned.1.call-start = ((), (), s32[]{:S(2)}) async-start(), calls=%async_computation.4 | async-start | bytes 262144 | tf_op jit(solution)/shard_map/psum | solution.py:63
  (34 other events, 45.8 us)
Sparse Core Ops, SparseCore 0:
  9.9 30.4 all-gather.3
  42.3 23.3 all-gather.5
  197.5 34.6 all-reduce.3
  270.2 22.1 all-gather.7
  296.3 34.6 all-reduce.5
where the time goes:
time: 378 us; the launch traced here: 375 us
  waiting for transfers between devices  112 us (30%)
  other arithmetic  102 us (27%)
  blocking collectives  54.6 us (14%)
  local copies, waits for them, and re-layouts  39.1 us (10%)
  loops' own time  26.2 us (7%)
  matrix products  26 us (7%)
  between operations  14.5 us (4%)
    psum x2, waiting for transfers between devices, per_device(): mapped = lax.psum(column_terms, 'shift')  69.5 us
    psum x2, blocking collectives, per_device(): gram_matrix = lax.psum(local_gram, 'row')  44.7 us
    sub x24, other arithmetic, make_some(): difference = window - mirror  28.7 us
    another operation x1, loops' own time, per_device(): lax.fori_loop(0, every_offset.shape[0], add_block, jnp.zeros((block_rows,...  26.2 us
    convert_element_type x24, other arithmetic, make_some(): lax.dynamic_slice_in_dim(extended, offset + M - start - count, count, 0)  26 us
    all_gather x1, waiting for transfers between devices, per_device(): basis_rows = lax.all_gather(own_basis, 'row', axis=1, tiled=True)  22.3 us
    while x120, local copies, waits for them, and re-layouts  19.4 us
    all_gather x1, waiting for transfers between devices, per_device(): gathered = lax.all_gather(snapshots, 'row', axis=0, tiled=True)  19 us
  transfers between devices with their start and end apart: 5, of which 4 were waited for; matrix products, arithmetic and copies ran while one was open for 29% of the time, Pallas kernels for 0%

commit v1 on v0

--- a/solution.py
+++ b/solution.py
@@ -62,7 +62,11 @@
         )
         mapped = lax.psum(column_terms, "shift")
         local_gram = jnp.dot(mapped, mapped.T, precision=lax.Precision.HIGHEST)
-        gram_matrix = lax.psum(local_gram, "row")
+        gram_matrix = local_gram
+        for hop in (1, 2, 4):
+            gram_matrix = gram_matrix + lax.ppermute(
+                gram_matrix, "row", [(dev, dev ^ hop) for dev in range(8)]
+            )
         own_basis = jnp.dot(factor(gram_matrix), mapped, precision=lax.Precision.HIGHEST)
         if sweep + 1 < ITERS:
             basis_rows = lax.all_gather(own_basis, "row", axis=1, tiled=True)

time: 378 us -> 349 us (0.923)
  blocking collectives: 54.6 us -> 9.92 us
  waiting for transfers between devices: 112 us -> 125 us
  starting transfers between devices: 0.2 us -> 6.33 us
    psum x2 -> x0, blocking collectives: 44.7 us -> none  [per_device(): gram_matrix = lax.psum(local_gram, 'row')]
    ppermute x0 -> x6, waiting for transfers between devices: none -> 12.2 us  [per_device(): lax.ppermute(gram_matrix, 'row', [(dev, dev ^ hop) for dev in range(8)])]
    ppermute x0 -> x6, starting transfers between devices: none -> 5.95 us  [per_device(): lax.ppermute(gram_matrix, 'row', [(dev, dev ^ hop) for dev in range(8)])]
  transfers between devices with their start and end apart: 5 -> 11, of which waited for: 4 -> 10; matrix products, arithmetic and copies ran while one was open for 29% -> 32% of each run, Pallas kernels for 0% -> 0%
where the time goes in v1:
time: 349 us; the launch traced here: 347 us
  waiting for transfers between devices  125 us (36%)
  other arithmetic  103 us (30%)
  local copies, waits for them, and re-layouts  38.9 us (11%)
  matrix products  26 us (7%)
  loops' own time  23.5 us (7%)
  between operations  14.6 us (4%)
  blocking collectives  9.92 us (3%)
  starting transfers between devices  6.33 us (2%)
    psum x2, waiting for transfers between devices, per_device(): mapped = lax.psum(column_terms, 'shift')  69.5 us
    sub x24, other arithmetic, make_some(): difference = window - mirror  28.7 us
    convert_element_type x24, other arithmetic, make_some(): lax.dynamic_slice_in_dim(extended, offset + M - start - count, count, 0)  26 us
    another operation x1, loops' own time, per_device(): lax.fori_loop(0, every_offset.shape[0], add_block, jnp.zeros((block_rows,...  23.5 us
    all_gather x1, waiting for transfers between devices, per_device(): basis_rows = lax.all_gather(own_basis, 'row', axis=1, tiled=True)  23 us
    while x120, local copies, waits for them, and re-layouts  19.4 us
    all_gather x1, waiting for transfers between devices, per_device(): gathered = lax.all_gather(snapshots, 'row', axis=0, tiled=True)  18.9 us
    squeeze x24, other arithmetic, make_some(): bottom = jnp.concatenate([difference[:, 1], -difference[:, 0]], axis=1)  15.2 us
  transfers between devices with their start and end apart: 11, of which 10 were waited for; matrix products, arithmetic and copies ran while one was open for 32% of the time, Pallas kernels for 0%

profile of v1, /device:TPU:0, one launch (start us, length us, event | category | flops | bytes accessed | tf_op | source)
XLA Modules:
  0.0 346.9 jit_solution(15807779420143278547)
XLA Ops:
  11.6 9.9 %all-reduce = s32[12]{0:T(128)S(1)} all-reduce(s32[12]{0:T(128)S(1)} %dynamic-update-slice.2), channel_id=1, replica_groups=mesh['row'=8,'shift'=4] {'shift'}, use_global_device_ids=true, to_apply=%add | all-reduce | flops 12 | bytes 96
  21.5 18.9 %all-gather.4.cloned.1.call-done = bf16[4096,2,128]{2,1,0:T(2,128)(2,1)} async-done(((bf16[512,2,128]{2,1,0:T(2,128)(2,1)}), bf16[4096,2,128]{2,1,0:T(2,128)(2,1)}) %all-gather.4.cloned.1.call-update) | async-done | bytes 2097168 | tf_op jit(solution)/shard_map/all_gather | solution.py:38
  40.4 6.4 %pad_maximum_fusion = bf16[4224,2,128]{2,1,0:T(2,128)(2,1)S(1)} fusion(bf16[128,2,128]{2,1,0:T(2,128)(2,1)} %param.10, bf16[4096,2,128]{2,1,0:T(2,128)(2,1)} %all-gather.4.cloned.1.call-done), kind=kLoop, calls=%fused_computation.31 | loop fusion | flops 1081344 | bytes 4325376 | tf_op jit(solution)/shard_map/concatenate | solution.py:39
  46.8 1.6 copy.34
  48.4 140.2 %while.18 = (s32[]{:T(128)}, f32[512,1024]{1,0:T(8,128)}, s32[]{:T(128)}, s32[12]{0:T(128)S(1)}, bf16[4224,2,128]{2,0,1:T(8,128)(2,1)}, /*index=5*/s32[]{:T(128)...) while((s32[]{:T(128)}, f32[512,1024]{1,0:T(8,128)}, ...), condition=%wide.region_1.2_spmd.clone, body=%wide.region_0.1_spmd.clone.sunk | while | flops 273222688 | bytes 47713820 | solution.py:52
  58.8 1.3 copy-done.1
  93.9 1.3 copy-done.1
  117.3 1.3 copy-done.1
  140.6 1.3 copy-done.1
  152.3 1.3 copy-done.1
  175.7 1.3 copy-done.1
  187.4 1.3 copy-done.1
  188.7 1.8 broadcast_multiply_fusion
  190.5 4.0 %fusion.16 = f32[64,512]{1,0:T(8,128)} fusion(f32[512,1024]{1,0:T(8,128)S(1)} %broadcast_multiply_fusion, f32[64,4096]{1,0:T(8,128)} %all-gather.6.cloned.1.call-done, s32[]{:T(128)S(6)} %select_n.96), kind=kOutput, calls=%fused_computation.35 | convolution fusion | flops 402653184 | bytes 2490372 | tf_op jit(solution)/shard_map/dot_general | solution.py:60
  194.6 34.7 %all-reduce.4.cloned.1.call-done = f32[64,512]{1,0:T(8,128)} async-done(((f32[64,512]{1,0:T(8,128)}), f32[64,512]{1,0:T(8,128)}) %all-reduce.4.cloned.1.call-update) | async-done | bytes 131088 | tf_op jit(solution)/shard_map/psum | solution.py:63
  231.8 1.5 collective-permute-start.1
  233.3 2.5 collective-permute-done.1
  235.8 1.5 collective-permute-start.2
  237.2 2.5 collective-permute-done.2
  239.8 5.8 %cholesky.44 = f32[64,64]{1,0:T(8,128)S(1)} custom-call(f32[64,64]{1,0:T(8,128)S(1)} %fusion.27), custom_call_target="Cholesky" | custom-call | tf_op jit(solution)/shard_map/jit(cholesky)/cholesky | solution.py:27
  247.0 4.9 %custom-call.7 = f32[1,64,64]{1,2,0:T(8,128)S(1)} custom-call(f32[1,64,64]{2,1,0:T(8,128)S(1)} %fusion.22), custom_call_target="InvertDiagBlocksLowerTriangular" | custom-call | tf_op jit(solution)/shard_map/jit(_solve_triangular)/triangular_solve | solution.py:29
  252.1 1.8 fusion.33
  254.2 23.0 %all-gather.8.cloned.1.call-done = f32[64,4096]{1,0:T(8,128)} async-done(((f32[64,512]{1,0:T(8,128)}), f32[64,4096]{1,0:T(8,128)}) %all-gather.8.cloned.1.call-update) | async-done | bytes 1048592 | tf_op jit(solution)/shard_map/all_gather | solution.py:72
  277.2 3.7 %fusion.14 = f32[64,512]{1,0:T(8,128)} fusion(f32[512,1024]{1,0:T(8,128)S(1)} %broadcast_multiply_fusion, f32[64,4096]{1,0:T(8,128)} %all-gather.8.cloned.1.call-done, s32[]{:T(128)S(6)} %select_n.96), kind=kOutput, calls=%fused_computation.33 | convolution fusion | flops 402653184 | bytes 2490372 | tf_op jit(solution)/shard_map/dot_general | solution.py:60
  280.9 34.8 %all-reduce.6.cloned.1.call-done = f32[64,512]{1,0:T(8,128)} async-done(((f32[64,512]{1,0:T(8,128)}), f32[64,512]{1,0:T(8,128)}) %all-reduce.6.cloned.1.call-update) | async-done | bytes 131088 | tf_op jit(solution)/shard_map/psum | solution.py:63
  318.3 1.4 collective-permute-start.4
  319.7 2.5 collective-permute-done.4
  322.2 1.5 collective-permute-start.5
  323.6 2.5 collective-permute-done.5
  326.2 5.8 %cholesky.55 = f32[64,64]{1,0:T(8,128)S(1)} custom-call(f32[64,64]{1,0:T(8,128)S(1)} %fusion.25), custom_call_target="Cholesky" | custom-call | tf_op jit(solution)/shard_map/jit(cholesky)/cholesky | solution.py:27
  333.4 4.9 %custom-call.8 = f32[1,64,64]{1,2,0:T(8,128)S(1)} custom-call(f32[1,64,64]{2,1,0:T(8,128)S(1)} %fusion.23), custom_call_target="InvertDiagBlocksLowerTriangular" | custom-call | tf_op jit(solution)/shard_map/jit(_solve_triangular)/triangular_solve | solution.py:29
  338.6 1.8 fusion.35
  (298 shorter events, 119.9 us)
Async XLA Ops:
  7.2 33.2 %all-gather.4.cloned.1.call-start = ((), (), s32[]{:S(2)}) async-start(), calls=%async_computation | async-start | bytes 2359296 | tf_op jit(solution)/shard_map/all_gather | solution.py:38
  7.9 182.6 %all-gather.6.cloned.1.call-start = ((), (), s32[]{:S(2)}) async-start(), calls=%async_computation.1 | async-start | bytes 1179648 | tf_op jit(solution)/shard_map/all_gather | solution.py:56
  8.6 220.7 %all-reduce.4.cloned.1.call-start = ((), (), s32[]{:S(2)}) async-start(), calls=%async_computation.2 | async-start | bytes 262144 | tf_op jit(solution)/shard_map/psum | solution.py:63
  55.5 2.0 copy-start
  56.3 1.6 copy-start.4
  67.2 2.0 copy-start
  68.0 1.6 copy-start.4
  78.9 2.0 copy-start
  79.7 1.6 copy-start.4
  90.6 2.0 copy-start
  91.3 1.6 copy-start.4
  102.3 2.0 copy-start
  103.0 1.6 copy-start.4
  114.0 2.0 copy-start
  114.7 1.6 copy-start.4
  125.6 2.0 copy-start
  126.4 1.6 copy-start.4
  137.3 2.0 copy-start
  149.0 2.0 copy-start
  160.7 2.0 copy-start
  161.4 1.6 copy-start.4
  172.4 2.0 copy-start
  184.1 2.0 copy-start
  190.5 90.4 %copy-start.5 = (f32[512,1024]{1,0:T(8,128)}, f32[512,1024]{1,0:T(8,128)S(1)}, u32[]{:S(2)}) copy-start(f32[512,1024]{1,0:T(8,128)S(1)} %broadcast_multiply_fusion) | copy-start | bytes 6291460
  194.5 82.7 %all-gather.8.cloned.1.call-start = ((), (), s32[]{:S(2)}) async-start(), calls=%async_computation.3 | async-start | bytes 1179648 | tf_op jit(solution)/shard_map/all_gather | solution.py:72
  230.6 1.3 collective-permute-start
  231.8 3.9 %collective-permute-start.1 = (f32[64,64]{0,1:T(8,128)S(1)}, f32[64,64]{0,1:T(8,128)S(1)}, u32[]{:S(2)}, u32[]{:S(2)}) collective-permute-start(f32[64,64]{0,1:T(8,128)S(1)} %add.269), channel_id=1, source_target_pairs={{0,8},{4,12},{8,0},{12,4},{16,24},{20,28},{24,16},{28,20},{1,9},{5... | collective-permute-start | bytes 49160 | tf_op jit(solution)/shard_map/ppermute | solution.py:67
  235.8 3.9 %collective-permute-start.2 = (f32[64,64]{0,1:T(8,128)S(1)}, f32[64,64]{0,1:T(8,128)S(1)}, u32[]{:S(2)}, u32[]{:S(2)}) collective-permute-start(f32[64,64]{0,1:T(8,128)S(1)} %add.270), channel_id=1, source_target_pairs={{0,16},{4,20},{8,24},{12,28},{16,0},{20,4},{24,8},{28,12},{1,17},{... | collective-permute-start | bytes 49160 | tf_op jit(solution)/shard_map/ppermute | solution.py:67
  254.0 61.8 %all-reduce.6.cloned.1.call-start = ((), (), s32[]{:S(2)}) async-start(), calls=%async_computation.4 | async-start | bytes 262144 | tf_op jit(solution)/shard_map/psum | solution.py:63
  317.0 1.3 collective-permute-start.3
  318.3 3.9 %collective-permute-start.4 = (f32[64,64]{0,1:T(8,128)S(1)}, f32[64,64]{0,1:T(8,128)S(1)}, u32[]{:S(2)}, u32[]{:S(2)}) collective-permute-start(f32[64,64]{0,1:T(8,128)S(1)} %add.272), channel_id=1, source_target_pairs={{0,8},{4,12},{8,0},{12,4},{16,24},{20,28},{24,16},{28,20},{1,9},{5... | collective-permute-start | bytes 49160 | tf_op jit(solution)/shard_map/ppermute | solution.py:67
  322.2 3.9 %collective-permute-start.5 = (f32[64,64]{0,1:T(8,128)S(1)}, f32[64,64]{0,1:T(8,128)S(1)}, u32[]{:S(2)}, u32[]{:S(2)}) collective-permute-start(f32[64,64]{0,1:T(8,128)S(1)} %add.273), channel_id=1, source_target_pairs={{0,16},{4,20},{8,24},{12,28},{16,0},{20,4},{24,8},{28,12},{1,17},{... | collective-permute-start | bytes 49160 | tf_op jit(solution)/shard_map/ppermute | solution.py:67
  (40 other events, 54.9 us)
Sparse Core Ops, SparseCore 0:
  9.9 30.4 all-gather.3
  42.3 23.3 all-gather.5
  194.6 34.6 all-reduce.3
  254.1 23.0 all-gather.7
  281.1 34.6 all-reduce.5
